TPU v7x, 256 devices: a whole 4x4x8 slice. The times are simulated.
256 devices in a mesh: section: 32 (over z, y), dp: 4 (over x), mp: 2 (over core).
Axes of the slice: x: 4, y: 4, z: 8, core: 2. Of those that a mesh axis runs over, the one named last changes fastest.
Arguments:
- inputs: bfloat16 [4, 128, 8192], P(None, 'dp'), may hold values from -12.7 to 12.7
- value_weight: bfloat16 [32, 8192, 1024], P('section', None, 'mp'), may hold values from -0.13975425 to 0.13975425
- carry_gain: float32 [32, 8192], P('section'), may hold values from 0.6 to 1.4
- channel_bins: int32 [32, 8192], P('section'), may hold values from 0 to 15
- grid_picks: int32 [32, 20], P('section'), may hold values from 0 to 19, each once within a row
Outputs:
- quant_out: bfloat16 [32, 4, 128, 1024], P('section', None, 'dp', 'mp')
- grid_loss: float32 [32, 4], P('section')
Inputs may be any that keep to these rules, and one draw needn't show every extreme that they name: `grid_picks`: each row lists every grid point once.
All inputs are finite; a program needn't handle non-finite values.
Results may differ from a plain program's by a relative error of at most 0.029.
Values may be sent and summed in bfloat16 or wider, within the bound.
A program may use at most 192 MiB of HBM per device.

v0:
```python
import math
import jax
import jax.numpy as jnp
from jax import lax
from jax.sharding import PartitionSpec as P

D = 8192
KV = 1024
HEAD = 128
GROUP = 128
GRID = 20
PICKS = 4
EPS = 1e-06
LOSS_UNIT = 1000.0
TWO_PI = 2.0 * math.pi


def sent_to_all(value, axis):
    peers = lax.axis_size(axis)
    return lax.all_to_all(
        jnp.broadcast_to(value[None], (peers, *value.shape)), axis, 0, 0, tiled=True
    )


def over_copies(value, axis):
    everything = sent_to_all(value, axis)
    return jnp.sum(everything, axis=0)


def from_behind(block, axis, distance):
    devices = range(lax.axis_size(axis))
    route = [(i - distance, i) for i in devices if i - distance in devices]
    return lax.ppermute(block, axis, route)


def quantize(weight, channel_bin, grid_pick):
    exponent = grid_pick.astype(jnp.float32) / GRID
    scaling = jnp.exp2(exponent * channel_bin.astype(jnp.float32) / 4.0)
    scaled = weight.astype(jnp.float32) * scaling[:, None]
    blocks = scaled.reshape(scaled.shape[0] // GROUP, GROUP, scaled.shape[1])
    spacing = (jnp.max(jnp.abs(blocks), axis=1, keepdims=True) + EPS) / 7.0
    levels = blocks / spacing
    snapped = (levels - jnp.sin(TWO_PI * levels) / TWO_PI) * spacing
    return (snapped.reshape(scaled.shape) / scaling[:, None]).astype(jnp.bfloat16)


def repeat_heads(values):
    row_count, columns = values.shape
    head_view = values.reshape(row_count, columns // HEAD, 1, HEAD)
    spread = jnp.broadcast_to(head_view, (row_count, columns // HEAD, D // KV, HEAD))
    return spread.reshape(row_count, columns * (D // KV))


def local(inputs, value_weight, carry_gain, channel_bins, grid_picks):
    section_count = lax.axis_size("section")
    section_index = lax.axis_index("section")
    micro_count, row_count, model_width = inputs.shape
    weight = value_weight[0]
    gain_row = carry_gain[0]
    half_width = weight.shape[1]
    stacked = jnp.concatenate(
        [
            quantize(weight, channel_bins[0], grid_picks[0, pick_index])
            for pick_index in range(PICKS)
        ],
        axis=1,
    )
    residual_gain = 1.0 / math.sqrt(section_count)
    tick_count = section_count + micro_count - 1

    def grid_pass(stream):
        exact = jnp.dot(stream, weight, preferred_element_type=jnp.float32)
        candidate = jnp.dot(stream, stacked, preferred_element_type=jnp.float32).reshape(
            row_count, PICKS, half_width
        )
        errors = jnp.sum(jnp.square(candidate - exact[:, None, :]), axis=(0, 2))
        return (candidate[:, 0, :].astype(jnp.bfloat16), errors)

    def spare_pass(stream):
        return (jnp.zeros((row_count, half_width), jnp.bfloat16), jnp.zeros((PICKS,), jnp.float32))

    def advance(tick_index, state_tuple):
        received, outputs, totals = state_tuple
        slot_index = tick_index - section_index
        active = jnp.logical_and(slot_index >= 0, slot_index < micro_count)
        clamped = jnp.clip(slot_index, 0, micro_count - 1)
        entry_rows = lax.dynamic_index_in_dim(inputs, clamped, 0, keepdims=False)
        stream = jnp.where(section_index == 0, entry_rows, received)
        chosen, errors = lax.cond(active, grid_pass, spare_pass, stream)
        previous = lax.dynamic_index_in_dim(outputs, clamped, 0, keepdims=False)
        outputs = lax.dynamic_update_index_in_dim(
            outputs, jnp.where(active, chosen, previous), clamped, 0
        )
        totals = totals + over_copies(errors, ("dp", "mp"))
        part_width = model_width // lax.axis_size("mp")
        part_start = lax.axis_index("mp") * part_width
        own_features = lax.dynamic_slice_in_dim(stream, part_start, part_width, 1)
        own_gain = lax.dynamic_slice_in_dim(gain_row, part_start, part_width, 0)
        next_part = (
            own_features.astype(jnp.float32) * own_gain[None, :]
            + residual_gain * repeat_heads(chosen).astype(jnp.float32)
        ).astype(jnp.bfloat16)
        arrived = from_behind(next_part, "section", 1)
        received = lax.all_gather(arrived, "mp", axis=1, tiled=True)
        return (received, outputs, totals)

    initial = (
        jnp.zeros((row_count, model_width), jnp.bfloat16),
        jnp.zeros((micro_count, row_count, half_width), jnp.bfloat16),
        jnp.zeros((PICKS,), jnp.float32),
    )
    received, outputs, totals = lax.fori_loop(0, tick_count, advance, initial)
    entry_count = micro_count * row_count * lax.axis_size("dp") * half_width * lax.axis_size("mp")
    grid_loss = totals * LOSS_UNIT / entry_count
    return (outputs[None], grid_loss[None])


def solution(mesh):
    placed = (
        P(None, "dp", None),
        P("section", None, "mp"),
        P("section", None),
        P("section", None),
        P("section", None),
    )
    return jax.shard_map(
        local,
        mesh=mesh,
        in_specs=placed,
        out_specs=(P("section", None, "dp", "mp"), P("section", None)),
        check_vma=False,
    )
```

profile of v0, /device:TPU:241, one launch (start us, length us, event | category | flops | bytes accessed | tf_op | source)
XLA Modules:
  0.0 1432.9 jit_solution(17592622582749549896)
XLA Ops:
  5.6 12.4 fusion.11
  18.1 246.1 %fusion.3 = (bf16[8192,512]{1,0:T(8,128)(2,1)}, bf16[8192,512]{1,0:T(8,128)(2,1)}, bf16[8192,512]{1,0:T(8,128)(2,1)}, bf16[8192,512]{1,0:T(8,128)(2,1)}) fusion(f32[64,512]{1,0:T(8,128)S(1)} %get-tuple-element.292, f32[8192]{0:T(1024)S(1)} %bitcast.105, bf16[1,8192,512]{2,1,0:T(8,128)(2,1)} %param.10, f32[64,512]{1,0:T(8,128)S(1)} %get-tuple-element.289, ...), kind=kLoop, calls=%fused_computation.29 | loop fusion | flops 138412032 | bytes 42598400 | tf_op jit(solution)/shard_map/convert_element_type | solution.py:44
  264.2 22.7 %pad_maximum_fusion = bf16[8192,2048]{1,0:T(8,128)(2,1)} fusion(bf16[8192,512]{1,0:T(8,128)(2,1)} %get-tuple-element.278, bf16[8192,512]{1,0:T(8,128)(2,1)} %get-tuple-element.279, bf16[8192,512]{1,0:T(8,128)(2,1)} %get-tuple-element.280, bf16[8192,512]{1,0:T(8,128)(2,1)} %get-tuple-element.277), kind=kLoop, calls=%fused_computation.11 | loop fusion | flops 134217728 | bytes 67108864 | tf_op jit(solution)/shard_map/concatenate | solution.py:61
  287.0 1145.3 %while.19 = (s32[]{:T(128)}, bf16[32,8192]{1,0:T(8,128)(2,1)S(1)}, bf16[4,32,512]{2,1,0:T(8,128)(2,1)S(1)}, f32[4]{0:T(128)S(1)}, pred[]{:T(512)}, /*index=5*/s3...) while((s32[]{:T(128)}, bf16[32,8192]{1,0:T(8,128)(2,1)S(1)}, ...), condition=%wide.region_10.11_spmd.clone, body=%wide.region_4.10_spmd.clone.sunk | while | flops 1343275008 | bytes 50324384 | solution.py:112
  292.4 5.3 all-to-all-start
  371.7 4.5 all-to-all-done
  419.1 4.5 all-to-all-done
  435.3 4.5 all-to-all-done
  532.1 4.5 all-to-all-done
  548.2 4.5 all-to-all-done
  628.9 4.5 all-to-all-done
  645.0 4.5 all-to-all-done
  725.7 4.5 all-to-all-done
  762.5 490.0 %collective-permute-done = bf16[32,4096]{1,0:T(8,128)(2,1)S(1)} collective-permute-done((bf16[32,4096]{1,0:T(8,128)(2,1)S(1)}, bf16[32,4096]{1,0:T(8,128)(2,1)S(1)}, u32[]{:S(2)}, u32[]{:S(2)}) %collective-permute-start) | collective-permute-done | bytes 262176 | tf_op jit(solution)/shard_map/while/body/eval_jaxpr/ppermute | solution.py:33
  1256.4 19.0 %conditional.3 = (bf16[32,512]{1,0:T(8,128)(2,1)S(1)}, f32[4]{0:T(128)S(1)}, f32[32,512]{1,0:T(8,128)S(1)}) conditional(s32[]{:T(128)} %convert_element_type.178, () %tuple.72, (bf16[32,8192]{1,0:T(8,128)(2,1)S(1)}, bf16[8192,2048]{1,0:T(8,128)(2,1)}, bf16[8192,512]{1,0:T(8,128)(2,1)}) %tuple.73), branch_computations={%region_5.5_spmd, %region_6.8_spmd} | conditional | flops 1342455808 | bytes 44793900 | solution.py:89
  1256.4 4.9 fusion.20
  1261.5 13.6 multiply_reduce_fusion
  1278.3 4.9 all-to-all-start
  1292.6 19.0 %conditional.3 = (bf16[32,512]{1,0:T(8,128)(2,1)S(1)}, f32[4]{0:T(128)S(1)}, f32[32,512]{1,0:T(8,128)S(1)}) conditional(s32[]{:T(128)} %convert_element_type.178, () %tuple.72, (bf16[32,8192]{1,0:T(8,128)(2,1)S(1)}, bf16[8192,2048]{1,0:T(8,128)(2,1)}, bf16[8192,512]{1,0:T(8,128)(2,1)}) %tuple.73), branch_computations={%region_5.5_spmd, %region_6.8_spmd} | conditional | flops 1342455808 | bytes 44793900 | solution.py:89
  1292.7 4.9 fusion.20
  1297.7 13.6 multiply_reduce_fusion
  1314.6 4.9 all-to-all-start
  1328.9 19.0 %conditional.3 = (bf16[32,512]{1,0:T(8,128)(2,1)S(1)}, f32[4]{0:T(128)S(1)}, f32[32,512]{1,0:T(8,128)S(1)}) conditional(s32[]{:T(128)} %convert_element_type.178, () %tuple.72, (bf16[32,8192]{1,0:T(8,128)(2,1)S(1)}, bf16[8192,2048]{1,0:T(8,128)(2,1)}, bf16[8192,512]{1,0:T(8,128)(2,1)}) %tuple.73), branch_computations={%region_5.5_spmd, %region_6.8_spmd} | conditional | flops 1342455808 | bytes 44793900 | solution.py:89
  1328.9 4.9 fusion.20
  1334.0 13.6 multiply_reduce_fusion
  1350.8 4.9 all-to-all-start
  1365.1 19.0 %conditional.3 = (bf16[32,512]{1,0:T(8,128)(2,1)S(1)}, f32[4]{0:T(128)S(1)}, f32[32,512]{1,0:T(8,128)S(1)}) conditional(s32[]{:T(128)} %convert_element_type.178, () %tuple.72, (bf16[32,8192]{1,0:T(8,128)(2,1)S(1)}, bf16[8192,2048]{1,0:T(8,128)(2,1)}, bf16[8192,512]{1,0:T(8,128)(2,1)}) %tuple.73), branch_computations={%region_5.5_spmd, %region_6.8_spmd} | conditional | flops 1342455808 | bytes 44793900 | solution.py:89
  1365.2 4.9 fusion.20
  1370.2 13.6 multiply_reduce_fusion
  1387.1 4.9 all-to-all-start
  1400.7 18.7 %collective-permute-start = (bf16[32,4096]{1,0:T(8,128)(2,1)S(1)}, bf16[32,4096]{1,0:T(8,128)(2,1)S(1)}, u32[]{:S(2)}, u32[]{:S(2)}) collective-permute-start(bf16[32,4096]{1,0:T(8,128)(2,1)S(1)} %fusion.27), channel_id=1, source_target_pairs={{0,8},{8,16},{16,24},{24,32},{32,40},{40,48},{48,56},{56,64},{64,7... | collective-permute-start | bytes 786440 | tf_op jit(solution)/shard_map/while/body/eval_jaxpr/ppermute | solution.py:33
  1420.0 5.2 all-to-all-start
  (708 shorter events, 497.0 us)
Async XLA Ops:
  288.8 13.3 collective-permute-start
  321.1 10.7 collective-permute-start
  365.6 10.8 collective-permute-start
  380.7 11.8 collective-permute-start
  396.9 11.8 collective-permute-start
  413.0 11.8 collective-permute-start
  429.1 11.8 collective-permute-start
  445.3 11.8 collective-permute-start
  461.4 11.8 collective-permute-start
  477.5 11.8 collective-permute-start
  493.7 11.8 collective-permute-start
  509.8 11.8 collective-permute-start
  525.9 11.8 collective-permute-start
  542.1 11.8 collective-permute-start
  558.2 11.8 collective-permute-start
  574.3 11.8 collective-permute-start
  590.5 11.8 collective-permute-start
  606.6 11.8 collective-permute-start
  622.7 11.8 collective-permute-start
  638.9 11.8 collective-permute-start
  655.0 11.8 collective-permute-start
  671.2 11.8 collective-permute-start
  687.3 11.8 collective-permute-start
  703.4 11.8 collective-permute-start
  719.6 11.8 collective-permute-start
  735.7 11.8 collective-permute-start
  751.8 500.7 %collective-permute-start = (bf16[32,4096]{1,0:T(8,128)(2,1)S(1)}, bf16[32,4096]{1,0:T(8,128)(2,1)S(1)}, u32[]{:S(2)}, u32[]{:S(2)}) collective-permute-start(bf16[32,4096]{1,0:T(8,128)(2,1)S(1)} %fusion.27), channel_id=1, source_target_pairs={{0,8},{8,16},{16,24},{24,32},{32,40},{40,48},{48,56},{56,64},{64,7... | collective-permute-start | bytes 786440 | tf_op jit(solution)/shard_map/while/body/eval_jaxpr/ppermute | solution.py:33
  1275.8 13.0 collective-permute-start
  1312.1 13.0 collective-permute-start
  1348.3 13.0 collective-permute-start
  1384.6 12.0 collective-permute-start
  1400.7 29.1 %collective-permute-start = (bf16[32,4096]{1,0:T(8,128)(2,1)S(1)}, bf16[32,4096]{1,0:T(8,128)(2,1)S(1)}, u32[]{:S(2)}, u32[]{:S(2)}) collective-permute-start(bf16[32,4096]{1,0:T(8,128)(2,1)S(1)} %fusion.27), channel_id=1, source_target_pairs={{0,8},{8,16},{16,24},{24,32},{32,40},{40,48},{48,56},{56,64},{64,7... | collective-permute-start | bytes 786440 | tf_op jit(solution)/shard_map/while/body/eval_jaxpr/ppermute | solution.py:33
  (40 other events, 348.6 us)
where the time goes:
time: 1440 us; the launch traced here: 1430 us
  waiting for transfers between devices  676 us (47%)
  other arithmetic  335 us (23%)
  starting transfers between devices  219 us (15%)
  blocking collectives  94.4 us (7%)
  matrix products  74 us (5%)
  local copies, waits for them, and re-layouts  27.1 us (2%)
    ppermute x35, waiting for transfers between devices, from_behind(): return lax.ppermute(block, axis, route)  518 us
    convert_element_type x1, other arithmetic, quantize(): (snapped.reshape(scaled.shape) / scaling[:, None]).astype(jnp.bfloat16)  246 us
    all_to_all x35, waiting for transfers between devices, sent_to_all(): lax.all_to_all(jnp.broadcast_to(value[None], (peers, *value.shape)), axis...  158 us
    all_to_all x35, starting transfers between devices, sent_to_all(): lax.all_to_all(jnp.broadcast_to(value[None], (peers, *value.shape)), axis...  134 us
    all_gather x35, blocking collectives, advance(): received = lax.all_gather(arrived, 'mp', axis=1, tiled=True)  94.4 us
    ppermute x35, starting transfers between devices, from_behind(): return lax.ppermute(block, axis, route)  85 us
    dot_general x4, matrix products, grid_pass(): jnp.dot(stream, stacked, preferred_element_type=jnp.float32)  54.4 us
    select_n x35, other arithmetic, advance(): stream = jnp.where(section_index == 0, entry_rows, received)  38.4 us
  transfers between devices with their start and end apart: 70, of which 63 were waited for; matrix products, arithmetic and copies ran while one was open for 2% of the time, Pallas kernels for 0%

commit v1 on v0

--- a/solution.py
+++ b/solution.py
@@ -101,7 +101,8 @@
             + residual_gain * repeat_heads(chosen).astype(jnp.float32)
         ).astype(jnp.bfloat16)
         arrived = from_behind(next_part, "section", 1)
-        received = lax.all_gather(arrived, "mp", axis=1, tiled=True)
+        outgoing = jnp.stack([arrived] * lax.axis_size("mp"))
+        received = jnp.concatenate(lax.all_to_all(outgoing, "mp", 0, 0), axis=1)
         return (received, outputs, totals)
 
     initial = (

time: 1440 us -> 1510 us (1.049)
  blocking collectives: 94.4 us -> 164 us
    all_to_all x0 -> x35, blocking collectives: none -> 164 us  [advance(): received = jnp.concatenate(lax.all_to_all(outgoing, 'mp', 0, 0), axis=1)]
    all_gather x35 -> x0, blocking collectives: 94.4 us -> none  [advance(): received = lax.all_gather(arrived, 'mp', axis=1, tiled=True)]
where the time goes in v1:
time: 1510 us
  waiting for transfers between devices  676 us (45%)
  other arithmetic  337 us (22%)
  starting transfers between devices  219 us (15%)
  blocking collectives  164 us (11%)
  matrix products  74 us (5%)
  local copies, waits for them, and re-layouts  28.3 us (2%)
    ppermute x35, waiting for transfers between devices, from_behind(): return lax.ppermute(block, axis, route)  518 us
    convert_element_type x1, other arithmetic, quantize(): (snapped.reshape(scaled.shape) / scaling[:, None]).astype(jnp.bfloat16)  246 us
    all_to_all x35, blocking collectives, advance(): received = jnp.concatenate(lax.all_to_all(outgoing, 'mp', 0, 0), axis=1)  164 us
    all_to_all x35, waiting for transfers between devices, sent_to_all(): lax.all_to_all(jnp.broadcast_to(value[None], (peers, *value.shape)), axis...  158 us
    all_to_all x35, starting transfers between devices, sent_to_all(): lax.all_to_all(jnp.broadcast_to(value[None], (peers, *value.shape)), axis...  134 us
    ppermute x35, starting transfers between devices, from_behind(): return lax.ppermute(block, axis, route)  85 us
    dot_general x4, matrix products, grid_pass(): jnp.dot(stream, stacked, preferred_element_type=jnp.float32)  54.4 us
    select_n x35, other arithmetic, advance(): stream = jnp.where(section_index == 0, entry_rows, received)  38.7 us
  transfers between devices with their start and end apart: 70, of which 63 were waited for; matrix products, arithmetic and copies ran while one was open for 2% of the time, Pallas kernels for 0%

profile of v1, /device:TPU:241, one launch (start us, length us, event | category | flops | bytes accessed | tf_op | source)
XLA Modules:
  0.0 1506.5 jit_solution(8149324114972896499)
XLA Ops:
  5.6 12.4 fusion.11
  18.1 246.1 %fusion.3 = (bf16[8192,512]{1,0:T(8,128)(2,1)}, bf16[8192,512]{1,0:T(8,128)(2,1)}, bf16[8192,512]{1,0:T(8,128)(2,1)}, bf16[8192,512]{1,0:T(8,128)(2,1)}) fusion(f32[64,512]{1,0:T(8,128)S(1)} %get-tuple-element.292, f32[8192]{0:T(1024)S(1)} %bitcast.118, bf16[1,8192,512]{2,1,0:T(8,128)(2,1)} %param.10, f32[64,512]{1,0:T(8,128)S(1)} %get-tuple-element.289, ...), kind=kLoop, calls=%fused_computation.30 | loop fusion | flops 138412032 | bytes 42598400 | tf_op jit(solution)/shard_map/convert_element_type | solution.py:44
  264.2 22.7 %pad_maximum_fusion.1 = bf16[8192,2048]{1,0:T(8,128)(2,1)} fusion(bf16[8192,512]{1,0:T(8,128)(2,1)} %get-tuple-element.278, bf16[8192,512]{1,0:T(8,128)(2,1)} %get-tuple-element.279, bf16[8192,512]{1,0:T(8,128)(2,1)} %get-tuple-element.280, bf16[8192,512]{1,0:T(8,128)(2,1)} %get-tuple-element.277), kind=kLoop, calls=%fused_computation.12 | loop fusion | flops 134217728 | bytes 67108864 | tf_op jit(solution)/shard_map/concatenate | solution.py:61
  287.0 1218.8 %while.19 = (s32[]{:T(128)}, bf16[32,8192]{1,0:T(8,128)(2,1)S(1)}, bf16[4,32,512]{2,1,0:T(8,128)(2,1)S(1)}, f32[4]{0:T(128)S(1)}, pred[]{:T(512)}, /*index=5*/s3...) while((s32[]{:T(128)}, bf16[32,8192]{1,0:T(8,128)(2,1)S(1)}, ...), condition=%wide.region_10.11_spmd.clone, body=%wide.region_4.10_spmd.clone.sunk | while | flops 1343537152 | bytes 52421536 | solution.py:113
  292.4 5.3 all-to-all-start.1
  386.9 4.7 all_to_all.25
  405.2 4.7 all_to_all.25
  423.4 4.7 all_to_all.25
  441.6 4.7 all_to_all.25
  459.9 4.7 all_to_all.25
  478.1 4.7 all_to_all.25
  496.3 4.7 all_to_all.25
  514.6 4.7 all_to_all.25
  823.5 490.0 %collective-permute-done = bf16[32,4096]{1,0:T(8,128)(2,1)S(1)} collective-permute-done((bf16[32,4096]{1,0:T(8,128)(2,1)S(1)}, bf16[32,4096]{1,0:T(8,128)(2,1)S(1)}, u32[]{:S(2)}, u32[]{:S(2)}) %collective-permute-start) | collective-permute-done | bytes 262176 | tf_op jit(solution)/shard_map/while/body/eval_jaxpr/ppermute | solution.py:33
  1319.5 19.0 %conditional.3 = (bf16[32,512]{1,0:T(8,128)(2,1)S(1)}, f32[4]{0:T(128)S(1)}, f32[32,512]{1,0:T(8,128)S(1)}) conditional(s32[]{:T(128)} %convert_element_type.178, () %tuple.72, (bf16[32,8192]{1,0:T(8,128)(2,1)S(1)}, bf16[8192,2048]{1,0:T(8,128)(2,1)}, bf16[8192,512]{1,0:T(8,128)(2,1)}) %tuple.73), branch_computations={%region_5.5_spmd, %region_6.8_spmd} | conditional | flops 1342455808 | bytes 44793900 | solution.py:89
  1319.5 4.9 fusion.20
  1324.6 13.6 multiply_reduce_fusion
  1341.4 4.9 all-to-all-start.1
  1357.8 19.0 %conditional.3 = (bf16[32,512]{1,0:T(8,128)(2,1)S(1)}, f32[4]{0:T(128)S(1)}, f32[32,512]{1,0:T(8,128)S(1)}) conditional(s32[]{:T(128)} %convert_element_type.178, () %tuple.72, (bf16[32,8192]{1,0:T(8,128)(2,1)S(1)}, bf16[8192,2048]{1,0:T(8,128)(2,1)}, bf16[8192,512]{1,0:T(8,128)(2,1)}) %tuple.73), branch_computations={%region_5.5_spmd, %region_6.8_spmd} | conditional | flops 1342455808 | bytes 44793900 | solution.py:89
  1357.9 4.9 fusion.20
  1362.9 13.6 multiply_reduce_fusion
  1379.8 4.9 all-to-all-start.1
  1396.2 19.0 %conditional.3 = (bf16[32,512]{1,0:T(8,128)(2,1)S(1)}, f32[4]{0:T(128)S(1)}, f32[32,512]{1,0:T(8,128)S(1)}) conditional(s32[]{:T(128)} %convert_element_type.178, () %tuple.72, (bf16[32,8192]{1,0:T(8,128)(2,1)S(1)}, bf16[8192,2048]{1,0:T(8,128)(2,1)}, bf16[8192,512]{1,0:T(8,128)(2,1)}) %tuple.73), branch_computations={%region_5.5_spmd, %region_6.8_spmd} | conditional | flops 1342455808 | bytes 44793900 | solution.py:89
  1396.2 4.9 fusion.20
  1401.3 13.6 multiply_reduce_fusion
  1418.1 4.9 all-to-all-start.1
  1434.5 19.0 %conditional.3 = (bf16[32,512]{1,0:T(8,128)(2,1)S(1)}, f32[4]{0:T(128)S(1)}, f32[32,512]{1,0:T(8,128)S(1)}) conditional(s32[]{:T(128)} %convert_element_type.178, () %tuple.72, (bf16[32,8192]{1,0:T(8,128)(2,1)S(1)}, bf16[8192,2048]{1,0:T(8,128)(2,1)}, bf16[8192,512]{1,0:T(8,128)(2,1)}) %tuple.73), branch_computations={%region_5.5_spmd, %region_6.8_spmd} | conditional | flops 1342455808 | bytes 44793900 | solution.py:89
  1434.6 4.9 fusion.20
  1439.6 13.6 multiply_reduce_fusion
  1456.5 4.9 all-to-all-start.1
  1472.2 18.7 %collective-permute-start = (bf16[32,4096]{1,0:T(8,128)(2,1)S(1)}, bf16[32,4096]{1,0:T(8,128)(2,1)S(1)}, u32[]{:S(2)}, u32[]{:S(2)}) collective-permute-start(bf16[32,4096]{1,0:T(8,128)(2,1)S(1)} %fusion.27), channel_id=1, source_target_pairs={{0,8},{8,16},{16,24},{24,32},{32,40},{40,48},{48,56},{56,64},{64,7... | collective-permute-start | bytes 786440 | tf_op jit(solution)/shard_map/while/body/eval_jaxpr/ppermute | solution.py:33
  1491.5 5.2 all-to-all-start.1
  (778 shorter events, 567.5 us)
Async XLA Ops:
  288.8 13.3 collective-permute-start
  308.4 10.7 collective-permute-start
  376.1 10.8 collective-permute-start
  393.3 11.8 collective-permute-start
  411.6 11.8 collective-permute-start
  429.8 11.8 collective-permute-start
  448.1 11.8 collective-permute-start
  466.3 11.8 collective-permute-start
  484.5 11.8 collective-permute-start
  502.8 11.8 collective-permute-start
  521.0 11.8 collective-permute-start
  539.2 11.8 collective-permute-start
  557.5 11.8 collective-permute-start
  575.7 11.8 collective-permute-start
  594.0 11.8 collective-permute-start
  612.2 11.8 collective-permute-start
  630.4 11.8 collective-permute-start
  648.7 11.8 collective-permute-start
  666.9 11.8 collective-permute-start
  685.2 11.8 collective-permute-start
  703.4 11.8 collective-permute-start
  721.6 11.8 collective-permute-start
  739.9 11.8 collective-permute-start
  758.1 11.8 collective-permute-start
  776.4 11.8 collective-permute-start
  794.6 11.8 collective-permute-start
  812.8 500.7 %collective-permute-start = (bf16[32,4096]{1,0:T(8,128)(2,1)S(1)}, bf16[32,4096]{1,0:T(8,128)(2,1)S(1)}, u32[]{:S(2)}, u32[]{:S(2)}) collective-permute-start(bf16[32,4096]{1,0:T(8,128)(2,1)S(1)} %fusion.27), channel_id=1, source_target_pairs={{0,8},{8,16},{16,24},{24,32},{32,40},{40,48},{48,56},{56,64},{64,7... | collective-permute-start | bytes 786440 | tf_op jit(solution)/shard_map/while/body/eval_jaxpr/ppermute | solution.py:33
  1338.9 13.0 collective-permute-start
  1377.3 13.0 collective-permute-start
  1415.6 13.0 collective-permute-start
  1454.0 12.0 collective-permute-start
  1472.2 29.1 %collective-permute-start = (bf16[32,4096]{1,0:T(8,128)(2,1)S(1)}, bf16[32,4096]{1,0:T(8,128)(2,1)S(1)}, u32[]{:S(2)}, u32[]{:S(2)}) collective-permute-start(bf16[32,4096]{1,0:T(8,128)(2,1)S(1)} %fusion.27), channel_id=1, source_target_pairs={{0,8},{8,16},{16,24},{24,32},{32,40},{40,48},{48,56},{56,64},{64,7... | collective-permute-start | bytes 786440 | tf_op jit(solution)/shard_map/while/body/eval_jaxpr/ppermute | solution.py:33
  (40 other events, 348.6 us)
